TPU v7x, 32 devices: a whole 2x2x4 slice. The times are simulated.
32 devices in a mesh: groups: 2 (over x), gx: 8 (over z, y), gy: 2 (over core).
Axes of the slice: x: 2, y: 2, z: 4, core: 2. Of those that a mesh axis runs over, the one named last changes fastest.
Arguments:
- source: float32 [2, 3, 2, 32, 64, 256], P('groups', None, None, 'gx', 'gy'), parts along dimension 0, may hold values from -12 to 12
- permittivity: float32 [6, 32, 64, 256], P('groups', 'gx', 'gy'), parts along dimension 0, may hold values from 1 to 12
- frequency: float32 [1], replicated, may hold values from 0.25 to 0.6
Outputs:
- solution: float32 [2, 3, 2, 32, 64, 256], P('groups', None, None, 'gx', 'gy'), parts along dimension 0
- residual: float32 [2, 3, 2, 32, 64, 256], P('groups', None, None, 'gx', 'gy'), parts along dimension 0
There are 2 independent parts, one for each index of `groups`. A program takes and returns all parts, laid end to end along the dimension named above; an argument that names none is the same for every part. Nothing has to cross between parts.
All inputs are finite; a program needn't handle non-finite values.
Results may differ from a plain program's by a relative error of at most 0.0003.
Values sent between devices are 32-bit elements; how exact they have to be, the bound alone decides.
A program may use at most 64 MiB of HBM per device.

v0:
```python
import jax
import jax.numpy as jnp
from jax import lax
from jax.sharding import PartitionSpec as P

NZ = 256
PML = 8
ITERS = 3
pml_strength = 2.0


def shifted(array, axis, by):
    devices = lax.axis_size(axis)
    pairs = [(i, i + by) for i in range(devices) if 0 <= i + by < devices]
    return lax.ppermute(array, axis, pairs)


def stretch(points, length, frequency):
    inside = jnp.maximum(jnp.maximum(PML - points, points - (length - PML)), 0.0) / PML
    damping = pml_strength * inside**3 / frequency[:, None]
    factor = 1.0 / (1.0 + damping * damping)
    return jnp.stack([factor, -damping * factor], axis=1)


def orient(coefficient, dimension):
    target = [coefficient.shape[0], 2, 1, 1, 1]
    target[dimension] = coefficient.shape[2]
    return coefficient.reshape(target)


def times_coef(values, coefficient):
    real_part = values[:, 0] * coefficient[:, 0] - values[:, 1] * coefficient[:, 1]
    imag_part = values[:, 0] * coefficient[:, 1] + values[:, 1] * coefficient[:, 0]
    return jnp.stack([real_part, imag_part], axis=1)


def curl_forward(extended, front_x, front_y, front_z):
    centre = extended[:, :, :, :-1, :-1]

    def step_x(component):
        return extended[:, component, :, 1:, :-1] - centre[:, component]

    def step_y(component):
        return extended[:, component, :, :-1, 1:] - centre[:, component]

    def step_z(component):
        cells = centre[:, component]
        above = jnp.concatenate([cells[..., 1:], jnp.zeros_like(cells[..., :1])], axis=-1)
        return above - cells

    curl_x = times_coef(step_y(2), front_y) - times_coef(step_z(1), front_z)
    curl_y = times_coef(step_z(0), front_z) - times_coef(step_x(2), front_x)
    curl_z = times_coef(step_x(1), front_x) - times_coef(step_y(0), front_y)
    return jnp.stack([curl_x, curl_y, curl_z], axis=1)


def curl_backward(padded, back_x, back_y, back_z):
    centre = padded[:, :, :, 1:, 1:]

    def step_x(component):
        return centre[:, component] - padded[:, component, :, :-1, 1:]

    def step_y(component):
        return centre[:, component] - padded[:, component, :, 1:, :-1]

    def step_z(component):
        cells = centre[:, component]
        below = jnp.concatenate([jnp.zeros_like(cells[..., :1]), cells[..., :-1]], axis=-1)
        return cells - below

    out_x = times_coef(step_y(2), back_y) - times_coef(step_z(1), back_z)
    out_y = times_coef(step_z(0), back_z) - times_coef(step_x(2), back_x)
    out_z = times_coef(step_x(1), back_x) - times_coef(step_y(0), back_y)
    return jnp.stack([out_x, out_y, out_z], axis=1)


def scaled(values, number):
    real_scale = number[0].reshape(-1, 1, 1, 1, 1)
    imag_scale = number[1].reshape(-1, 1, 1, 1, 1)
    real_part = values[:, :, 0] * real_scale - values[:, :, 1] * imag_scale
    imag_part = values[:, :, 0] * imag_scale + values[:, :, 1] * real_scale
    return jnp.stack([real_part, imag_part], axis=2)


def product(left, right):
    real_part = jnp.sum(
        left[:, :, 0] * right[:, :, 0] + left[:, :, 1] * right[:, :, 1], axis=(1, 2, 3, 4)
    )
    imag_part = jnp.sum(
        left[:, :, 0] * right[:, :, 1] - left[:, :, 1] * right[:, :, 0], axis=(1, 2, 3, 4)
    )
    return jnp.stack([real_part, imag_part])


def complex_times(first, other):
    return jnp.stack(
        [first[0] * other[0] - first[1] * other[1], first[0] * other[1] + first[1] * other[0]]
    )


def complex_ratio(first, other):
    modulus = other[0] * other[0] + other[1] * other[1]
    return (
        jnp.stack(
            [first[0] * other[0] + first[1] * other[1], first[1] * other[0] - first[0] * other[1]]
        )
        / modulus
    )


def grid_points(start, first, count):
    return (start + jnp.arange(first, count, dtype=jnp.int32)).astype(jnp.float32)


def body(source, permittivity, frequency):
    cells_x = source.shape[3]
    cells_y = source.shape[4]
    total_x = cells_x * lax.axis_size("gx")
    total_y = cells_y * lax.axis_size("gy")
    index_x = lax.axis_index("gx")
    index_y = lax.axis_index("gy")
    margin = 0
    front_x = orient(
        stretch(grid_points(index_x * cells_x, -margin, cells_x) + 0.5, total_x, frequency), 2
    )
    front_y = orient(
        stretch(grid_points(index_y * cells_y, -margin, cells_y) + 0.5, total_y, frequency), 3
    )
    back_x = orient(stretch(grid_points(index_x * cells_x, 0, cells_x), total_x, frequency), 2)
    back_y = orient(stretch(grid_points(index_y * cells_y, 0, cells_y), total_y, frequency), 3)
    z_points = grid_points(0, 0, NZ)
    front_z = orient(stretch(z_points + 0.5, NZ, frequency), 4)
    back_z = orient(stretch(z_points, NZ, frequency), 4)
    material = (frequency * frequency).reshape(-1, 1, 1, 1, 1, 1) * permittivity[None, :, None]

    def operate(values):
        above_x = shifted(values[:, :, :, :1], "gx", -1)
        above_y = shifted(values[:, :, :, :, :1], "gy", -1)
        extended = jnp.concatenate([values, above_x], axis=3)
        side_cells = jnp.concatenate([above_y, jnp.zeros_like(above_y[:, :, :, :1])], axis=3)
        extended = jnp.concatenate([extended, side_cells], axis=4)
        rotated = curl_forward(extended, front_x, front_y, front_z)
        below_x = shifted(rotated[:, :, :, -1:], "gx", 1)
        below_y = shifted(rotated[:, :, :, :, -1:], "gy", 1)
        padded = jnp.concatenate([below_x, rotated], axis=3)
        side_cells = jnp.concatenate([jnp.zeros_like(below_y[:, :, :, :1]), below_y], axis=3)
        padded = jnp.concatenate([side_cells, padded], axis=4)
        applied = curl_backward(padded, back_x, back_y, back_z)
        return applied - material * values

    solution = jnp.zeros_like(source)
    residual = source
    direction = source
    shadow_dot = lax.psum(product(source, residual), ("gx", "gy"))
    for iteration in range(ITERS):
        applied = operate(direction)
        step_size = complex_ratio(shadow_dot, lax.psum(product(source, applied), ("gx", "gy")))
        middle = residual - scaled(applied, step_size)
        second = operate(middle)
        sums_triple = lax.psum(
            (product(second, middle), product(second, second), product(source, second)),
            ("gx", "gy"),
        )
        weight = complex_ratio(sums_triple[0], sums_triple[1])
        solution = solution + scaled(direction, step_size) + scaled(middle, weight)
        residual = middle - scaled(second, weight)
        if iteration + 1 < ITERS:
            shadow_next = -complex_times(weight, sums_triple[2])
            momentum = complex_times(
                complex_ratio(shadow_next, shadow_dot), complex_ratio(step_size, weight)
            )
            direction = residual + scaled(direction - scaled(applied, weight), momentum)
            shadow_dot = shadow_next
    return (solution, residual)


def solution(mesh):
    placed = (P("groups", None, None, "gx", "gy", None), P("groups", "gx", "gy", None), P())
    return jax.shard_map(
        body,
        mesh=mesh,
        in_specs=placed,
        out_specs=(
            P("groups", None, None, "gx", "gy", None),
            P("groups", None, None, "gx", "gy", None),
        ),
        check_vma=False,
    )
```

profile of v0, /device:TPU:0, one launch (start us, length us, event | category | flops | bytes accessed | tf_op | source)
XLA Modules:
  0.0 469.3 jit_solution(13969787863053648633)
XLA Ops:
  7.5 6.7 %collective-permute-done = f32[1,3,2,1,32,256]{5,4,3,2,1,0:T(8,128)S(1)} collective-permute-done((f32[1,3,2,1,32,256]{5,4,3,2,1,0:T(8,128)S(1)}, f32[1,3,2,1,32,256]{5,4,3,2,1,0:T(8,128)S(1)}, u32[]{:S(2)}, u32[]{:S(2)}) %collective-permute-start) | collective-permute-done | bytes 196640 | tf_op jit(solution)/shard_map/ppermute | solution.py:15
  15.4 2.2 collective-permute-start.2
  17.5 5.0 %collective-permute-start.3 = (f32[1,3,2,1,32,256]{5,4,3,2,1,0:T(8,128)S(1)}, f32[1,3,2,1,32,256]{5,4,3,2,1,0:T(8,128)S(1)}, u32[]{:S(2)}, u32[]{:S(2)}) collective-permute-start(f32[1,3,2,1,32,256]{5,4,3,2,1,0:T(8,128)S(1)} %pad_maximum_fusion.33), channel_id=1, source_target_pairs={{0,2},{2,4},{4,6},{6,8},{8,10},{10,12},{12,14},{1,3},{3,5},{5,7},{... | collective-permute-start | bytes 589832 | tf_op jit(solution)/shard_map/ppermute | solution.py:15
  22.5 3.6 collective-permute-done.3
  29.7 1.4 pad_maximum_fusion.41
  31.1 31.3 %all-reduce.39 = (f32[2,1]{1,0:T(2,128)S(1)}, f32[2,1]{1,0:T(2,128)S(1)}) all-reduce(f32[2,1]{1,0:T(2,128)S(1)} %pad_maximum_fusion.41, f32[2,1]{1,0:T(2,128)S(1)} %pad_maximum_fusion.42), channel_id=1, replica_groups=mesh['groups'=2,'gx'=8,'gy'=2] {'gx','gy'}, use_global_device_ids=true, to_apply=%region_2.0 | all-reduce | flops 4 | bytes 32 | tf_op jit(solution)/shard_map/psum | solution.py:154
  75.6 1.8 collective-permute-done.5
  77.4 3.2 collective-permute-done.4
  81.7 1.5 collective-permute-start.7
  83.2 1.7 collective-permute-start.6
  94.9 29.5 %all-reduce.38 = (f32[2,1]{1,0:T(2,128)S(1)}, f32[2,1]{1,0:T(2,128)S(1)}, f32[2,1]{1,0:T(2,128)S(1)}) all-reduce(f32[2,1]{1,0:T(2,128)S(1)} %pad_maximum_fusion.43, f32[2,1]{1,0:T(2,128)S(1)} %pad_maximum_fusion.44, f32[2,1]{1,0:T(2,128)S(1)} %pad_maximum_fusion.45), channel_id=1, replica_groups=mesh['groups'=2,'gx'=8,'gy'=2] {'gx','gy'}, use_global_device_ids=true, to_apply=%region_8.0 | all-reduce | flops 6 | bytes 48 | tf_op jit(solution)/shard_map/psum | solution.py:160
  141.5 2.5 multiply_subtract_fusion.11
  144.0 1.4 multiply_subtract_fusion.12
  166.5 1.8 collective-permute-done.9
  168.3 4.2 collective-permute-done.8
  173.6 1.5 collective-permute-start.11
  183.4 30.3 %psum.89 = f32[2,1]{1,0:T(2,128)S(1)} all-reduce(f32[2,1]{1,0:T(2,128)S(1)} %pad_maximum_fusion.46), channel_id=1, replica_groups=mesh['groups'=2,'gx'=8,'gy'=2] {'gx','gy'}, use_global_device_ids=true, to_apply=%region_17.0 | all-reduce | flops 2 | bytes 16 | tf_op jit(solution)/shard_map/psum | solution.py:157
  222.7 2.5 multiply_subtract_fusion.8
  226.9 1.5 collective-permute-start.13
  228.4 1.6 collective-permute-done.13
  230.0 3.4 collective-permute-done.12
  235.0 1.5 collective-permute-start.15
  236.5 1.5 collective-permute-start.14
  245.7 1.8 pad_maximum_fusion.49
  247.5 1.9 pad_maximum_fusion.48
  249.4 1.9 pad_maximum_fusion.47
  251.3 30.6 %all-reduce.37 = (f32[2,1]{1,0:T(2,128)}, f32[2,1]{1,0:T(2,128)}, f32[2,1]{1,0:T(2,128)}) all-reduce(f32[2,1]{1,0:T(2,128)} %pad_maximum_fusion.47, f32[2,1]{1,0:T(2,128)} %pad_maximum_fusion.48, f32[2,1]{1,0:T(2,128)} %pad_maximum_fusion.49), channel_id=1, replica_groups=mesh['groups'=2,'gx'=8,'gy'=2] {'gx','gy'}, use_global_device_ids=true, to_apply=%region_20.0 | all-reduce | flops 6 | bytes 48 | tf_op jit(solution)/shard_map/psum | solution.py:160
  300.1 2.5 multiply_subtract_fusion.5
  325.9 1.8 collective-permute-done.17
  327.7 3.7 collective-permute-done.16
  333.0 1.5 collective-permute-start.19
  336.7 1.7 collective-permute-done.19
  342.3 3.0 add_reduce_fusion.2
  345.3 1.8 pad_maximum_fusion.50
  347.1 2.3 multiply_subtract_fusion.13
  349.4 30.0 %psum.93 = f32[2,1]{1,0:T(2,128)S(1)} all-reduce(f32[2,1]{1,0:T(2,128)} %pad_maximum_fusion.50), channel_id=1, replica_groups=mesh['groups'=2,'gx'=8,'gy'=2] {'gx','gy'}, use_global_device_ids=true, to_apply=%region_29.0 | all-reduce | flops 2 | bytes 16 | tf_op jit(solution)/shard_map/psum | solution.py:157
  388.2 2.5 multiply_subtract_fusion.2
  390.7 2.3 maximum_subtract_fusion.11
  395.6 2.3 multiply_subtract_fusion.9
  397.9 5.9 %collective-permute-done.20 = f32[1,3,2,1,32,256]{5,4,3,2,1,0:T(8,128)S(1)} collective-permute-done((f32[1,3,2,1,32,256]{5,4,3,2,1,0:T(8,128)S(1)}, f32[1,3,2,1,32,256]{5,4,3,2,1,0:T(8,128)S(1)}, u32[]{:S(2)}, u32[]{:S(2)}) %collective-permute-start.20) | collective-permute-done | bytes 196640 | tf_op jit(solution)/shard_map/ppermute | solution.py:15
  405.4 2.0 collective-permute-start.22
  407.5 1.9 collective-permute-start.23
  409.3 2.2 multiply_subtract_fusion.7
  420.7 2.2 multiply_subtract_fusion.3
  422.9 29.5 %all-reduce.36 = (f32[2,1]{1,0:T(2,128)S(1)}, f32[2,1]{1,0:T(2,128)S(1)}) all-reduce(f32[2,1]{1,0:T(2,128)S(1)} %pad_maximum_fusion.51, f32[2,1]{1,0:T(2,128)S(1)} %pad_maximum_fusion.52), channel_id=1, replica_groups=mesh['groups'=2,'gx'=8,'gy'=2] {'gx','gy'}, use_global_device_ids=true, to_apply=%region_32.0 | all-reduce | flops 4 | bytes 32 | tf_op jit(solution)/shard_map/psum | solution.py:160
  461.4 2.6 multiply_subtract_fusion
  465.6 1.5 maximum_subtract_fusion.13
  467.9 1.4 fusion.3
  (439 shorter events, 87.4 us)
Async XLA Ops:
  1.6 12.5 %collective-permute-start.1 = (f32[1,3,2,4,1,256]{5,4,3,2,1,0:T(1,128)S(1)}, f32[1,3,2,4,1,256]{5,4,3,2,1,0:T(1,128)S(1)}, u32[]{:S(2)}, u32[]{:S(2)}) collective-permute-start(f32[1,3,2,4,1,256]{5,4,3,2,1,0:T(1,128)S(1)} %slice.702), channel_id=1, source_target_pairs={{1,0},{3,2},{5,4},{7,6},{9,8},{11,10},{13,12},{15,14},{17,16},{19,... | collective-permute-start | bytes 73736 | tf_op jit(solution)/shard_map/ppermute | solution.py:15
  3.9 10.2 %collective-permute-start = (f32[1,3,2,1,32,256]{5,4,3,2,1,0:T(8,128)S(1)}, f32[1,3,2,1,32,256]{5,4,3,2,1,0:T(8,128)S(1)}, u32[]{:S(2)}, u32[]{:S(2)}) collective-permute-start(f32[1,3,2,1,32,256]{5,4,3,2,1,0:T(8,128)S(1)} %slice.695), channel_id=1, source_target_pairs={{2,0},{4,2},{6,4},{8,6},{10,8},{12,10},{14,12},{3,1},{5,3},{7,5},{... | collective-permute-start | bytes 589832 | tf_op jit(solution)/shard_map/ppermute | solution.py:15
  7.1 172.1 %copy-start.53 = (f32[4]{0:T(128)}, f32[4]{0:T(128)S(1)}, u32[]{:S(2)}) copy-start(f32[4]{0:T(128)S(1)} %get-tuple-element.424) | copy-start | bytes 52
  7.1 172.1 %copy-start.57 = (f32[4]{0:T(128)}, f32[4]{0:T(128)S(1)}, u32[]{:S(2)}) copy-start(f32[4]{0:T(128)S(1)} %get-tuple-element.425) | copy-start | bytes 52
  7.2 166.2 %copy-start.61 = (f32[4]{0:T(128)}, f32[4]{0:T(128)S(1)}, u32[]{:S(2)}) copy-start(f32[4]{0:T(128)S(1)} %get-tuple-element.432) | copy-start | bytes 52
  7.2 166.2 %copy-start.65 = (f32[4]{0:T(128)}, f32[4]{0:T(128)S(1)}, u32[]{:S(2)}) copy-start(f32[4]{0:T(128)S(1)} %get-tuple-element.433) | copy-start | bytes 52
  7.4 172.3 %copy-start.16 = (f32[3,4,32,256]{3,2,1,0:T(8,128)}, f32[3,4,32,256]{3,2,1,0:T(8,128)S(1)}, u32[]{:S(2)}) copy-start(f32[3,4,32,256]{3,2,1,0:T(8,128)S(1)} %broadcast_multiply_fusion) | copy-start | bytes 1179652
  7.4 165.7 %copy-start.77 = (f32[32]{0:T(128)}, f32[32]{0:T(128)S(1)}, u32[]{:S(2)}) copy-start(f32[32]{0:T(128)S(1)} %get-tuple-element.430) | copy-start | bytes 388
  7.4 165.7 %copy-start.81 = (f32[32]{0:T(128)}, f32[32]{0:T(128)S(1)}, u32[]{:S(2)}) copy-start(f32[32]{0:T(128)S(1)} %get-tuple-element.431) | copy-start | bytes 388
  15.4 7.2 %collective-permute-start.2 = (f32[1,3,2,4,1,256]{5,4,3,2,1,0:T(1,128)S(1)}, f32[1,3,2,4,1,256]{5,4,3,2,1,0:T(1,128)S(1)}, u32[]{:S(2)}, u32[]{:S(2)}) collective-permute-start(f32[1,3,2,4,1,256]{5,4,3,2,1,0:T(1,128)S(1)} %pad_maximum_fusion.40), channel_id=1, source_target_pairs={{0,1},{2,3},{4,5},{6,7},{8,9},{10,11},{12,13},{14,15},{16,17},{18,... | collective-permute-start | bytes 73736 | tf_op jit(solution)/shard_map/ppermute | solution.py:15
  17.5 8.7 %collective-permute-start.3 = (f32[1,3,2,1,32,256]{5,4,3,2,1,0:T(8,128)S(1)}, f32[1,3,2,1,32,256]{5,4,3,2,1,0:T(8,128)S(1)}, u32[]{:S(2)}, u32[]{:S(2)}) collective-permute-start(f32[1,3,2,1,32,256]{5,4,3,2,1,0:T(8,128)S(1)} %pad_maximum_fusion.33), channel_id=1, source_target_pairs={{0,2},{2,4},{4,6},{6,8},{8,10},{10,12},{12,14},{1,3},{3,5},{5,7},{... | collective-permute-start | bytes 589832 | tf_op jit(solution)/shard_map/ppermute | solution.py:15
  22.5 156.8 %copy-start.69 = (f32[32]{0:T(128)}, f32[32]{0:T(128)S(1)}, u32[]{:S(2)}) copy-start(f32[32]{0:T(128)S(1)} %get-tuple-element.422) | copy-start | bytes 388
  22.5 156.8 %copy-start.73 = (f32[32]{0:T(128)}, f32[32]{0:T(128)S(1)}, u32[]{:S(2)}) copy-start(f32[32]{0:T(128)S(1)} %get-tuple-element.423) | copy-start | bytes 388
  27.5 45.4 %copy-start.27 = (f32[1,3,2,4,32,256]{5,4,3,2,1,0:T(8,128)}, f32[1,3,2,4,32,256]{5,4,3,2,1,0:T(8,128)S(1)}, u32[]{:S(2)}) copy-start(f32[1,3,2,4,32,256]{5,4,3,2,1,0:T(8,128)S(1)} %maximum_subtract_fusion) | copy-start | bytes 2359300
  73.0 7.6 %collective-permute-start.4 = (f32[1,3,2,1,32,256]{5,4,3,2,1,0:T(8,128)S(1)}, f32[1,3,2,1,32,256]{5,4,3,2,1,0:T(8,128)S(1)}, u32[]{:S(2)}, u32[]{:S(2)}) collective-permute-start(f32[1,3,2,1,32,256]{5,4,3,2,1,0:T(8,128)S(1)} %slice.2127), channel_id=1, source_target_pairs={{2,0},{4,2},{6,4},{8,6},{10,8},{12,10},{14,12},{3,1},{5,3},{7,5},{... | collective-permute-start | bytes 589832 | tf_op jit(solution)/shard_map/ppermute | solution.py:15
  74.3 3.1 collective-permute-start.5
  81.7 5.9 %collective-permute-start.7 = (f32[1,3,2,1,32,256]{5,4,3,2,1,0:T(8,128)S(1)}, f32[1,3,2,1,32,256]{5,4,3,2,1,0:T(8,128)S(1)}, u32[]{:S(2)}, u32[]{:S(2)}) collective-permute-start(f32[1,3,2,1,32,256]{5,4,3,2,1,0:T(8,128)S(1)} %pad_maximum_fusion.31), channel_id=1, source_target_pairs={{0,2},{2,4},{4,6},{6,8},{8,10},{10,12},{12,14},{1,3},{3,5},{5,7},{... | collective-permute-start | bytes 589832 | tf_op jit(solution)/shard_map/ppermute | solution.py:15
  83.2 4.4 collective-permute-start.6
  124.4 19.6 %copy-start.29 = (f32[1,3,2,4,32,256]{5,4,3,2,1,0:T(8,128)S(1)}, f32[1,3,2,4,32,256]{5,4,3,2,1,0:T(8,128)}, u32[]{:S(2)}) copy-start(f32[1,3,2,4,32,256]{5,4,3,2,1,0:T(8,128)} %copy-done.28) | copy-start | bytes 2359300
  145.4 34.3 %copy-start.1 = (f32[1,3,1,4,32,256]{5,4,3,2,1,0:T(8,128)}, f32[1,3,1,4,32,256]{5,4,3,2,1,0:T(8,128)S(1)}, u32[]{:S(2)}) copy-start(f32[1,3,1,4,32,256]{5,4,3,2,1,0:T(8,128)S(1)} %get-tuple-element.131) | copy-start | bytes 1179652
  163.5 16.2 %copy-start.34 = (f32[1,3,1,4,32,256]{5,4,3,2,1,0:T(8,128)}, f32[1,3,1,4,32,256]{5,4,3,2,1,0:T(8,128)S(1)}, u32[]{:S(2)}) copy-start(f32[1,3,1,4,32,256]{5,4,3,2,1,0:T(8,128)S(1)} %get-tuple-element.132) | copy-start | bytes 1179652
  163.5 16.2 %copy-start.36 = (f32[1,3,1,4,32,256]{5,4,3,2,1,0:T(8,128)}, f32[1,3,1,4,32,256]{5,4,3,2,1,0:T(8,128)S(1)}, u32[]{:S(2)}) copy-start(f32[1,3,1,4,32,256]{5,4,3,2,1,0:T(8,128)S(1)} %get-tuple-element.133) | copy-start | bytes 1179652
  163.9 8.6 %collective-permute-start.8 = (f32[1,3,2,1,32,256]{5,4,3,2,1,0:T(8,128)S(1)}, f32[1,3,2,1,32,256]{5,4,3,2,1,0:T(8,128)S(1)}, u32[]{:S(2)}, u32[]{:S(2)}) collective-permute-start(f32[1,3,2,1,32,256]{5,4,3,2,1,0:T(8,128)S(1)} %slice.2170), channel_id=1, source_target_pairs={{2,0},{4,2},{6,4},{8,6},{10,8},{12,10},{14,12},{3,1},{5,3},{7,5},{... | collective-permute-start | bytes 589832 | tf_op jit(solution)/shard_map/ppermute | solution.py:15
  165.2 3.1 collective-permute-start.9
  173.6 4.9 %collective-permute-start.11 = (f32[1,3,2,1,32,256]{5,4,3,2,1,0:T(8,128)S(1)}, f32[1,3,2,1,32,256]{5,4,3,2,1,0:T(8,128)S(1)}, u32[]{:S(2)}, u32[]{:S(2)}) collective-permute-start(f32[1,3,2,1,32,256]{5,4,3,2,1,0:T(8,128)S(1)} %pad_maximum_fusion.29), channel_id=1, source_target_pairs={{0,2},{2,4},{4,6},{6,8},{8,10},{10,12},{12,14},{1,3},{3,5},{5,7},{... | collective-permute-start | bytes 589832 | tf_op jit(solution)/shard_map/ppermute | solution.py:15
  175.1 2.1 collective-permute-start.10
  225.2 17.0 %copy-start.9 = (f32[1,3,1,4,32,256]{5,4,3,2,1,0:T(8,128)}, f32[1,3,1,4,32,256]{5,4,3,2,1,0:T(8,128)S(1)}, u32[]{:S(2)}) copy-start(f32[1,3,1,4,32,256]{5,4,3,2,1,0:T(8,128)S(1)} %get-tuple-element.118) | copy-start | bytes 1179652
  225.2 17.0 %copy-start.12 = (f32[1,3,1,4,32,256]{5,4,3,2,1,0:T(8,128)}, f32[1,3,1,4,32,256]{5,4,3,2,1,0:T(8,128)S(1)}, u32[]{:S(2)}) copy-start(f32[1,3,1,4,32,256]{5,4,3,2,1,0:T(8,128)S(1)} %get-tuple-element.119) | copy-start | bytes 1179652
  225.6 7.8 %collective-permute-start.12 = (f32[1,3,2,1,32,256]{5,4,3,2,1,0:T(8,128)S(1)}, f32[1,3,2,1,32,256]{5,4,3,2,1,0:T(8,128)S(1)}, u32[]{:S(2)}, u32[]{:S(2)}) collective-permute-start(f32[1,3,2,1,32,256]{5,4,3,2,1,0:T(8,128)S(1)} %slice.2211), channel_id=1, source_target_pairs={{2,0},{4,2},{6,4},{8,6},{10,8},{12,10},{14,12},{3,1},{5,3},{7,5},{... | collective-permute-start | bytes 589832 | tf_op jit(solution)/shard_map/ppermute | solution.py:15
  226.9 3.1 collective-permute-start.13
  235.0 5.6 %collective-permute-start.15 = (f32[1,3,2,1,32,256]{5,4,3,2,1,0:T(8,128)S(1)}, f32[1,3,2,1,32,256]{5,4,3,2,1,0:T(8,128)S(1)}, u32[]{:S(2)}, u32[]{:S(2)}) collective-permute-start(f32[1,3,2,1,32,256]{5,4,3,2,1,0:T(8,128)S(1)} %pad_maximum_fusion.27), channel_id=1, source_target_pairs={{0,2},{2,4},{4,6},{6,8},{8,10},{10,12},{12,14},{1,3},{3,5},{5,7},{... | collective-permute-start | bytes 589832 | tf_op jit(solution)/shard_map/ppermute | solution.py:15
  236.5 4.0 collective-permute-start.14
  281.9 20.7 %copy-start.31 = (f32[1,3,2,4,32,256]{5,4,3,2,1,0:T(8,128)S(1)}, f32[1,3,2,4,32,256]{5,4,3,2,1,0:T(8,128)}, u32[]{:S(2)}) copy-start(f32[1,3,2,4,32,256]{5,4,3,2,1,0:T(8,128)} %copy-done.30) | copy-start | bytes 2359300
  300.0 21.2 %copy-start.3 = (f32[1,3,1,4,32,256]{5,4,3,2,1,0:T(8,128)S(1)}, f32[1,3,1,4,32,256]{5,4,3,2,1,0:T(8,128)}, u32[]{:S(2)}) copy-start(f32[1,3,1,4,32,256]{5,4,3,2,1,0:T(8,128)} %copy-done.1) | copy-start | bytes 1179652
  300.0 21.2 %copy-start.35 = (f32[1,3,1,4,32,256]{5,4,3,2,1,0:T(8,128)S(1)}, f32[1,3,1,4,32,256]{5,4,3,2,1,0:T(8,128)}, u32[]{:S(2)}) copy-start(f32[1,3,1,4,32,256]{5,4,3,2,1,0:T(8,128)} %copy-done.34) | copy-start | bytes 1179652
  300.0 21.2 %copy-start.37 = (f32[1,3,1,4,32,256]{5,4,3,2,1,0:T(8,128)S(1)}, f32[1,3,1,4,32,256]{5,4,3,2,1,0:T(8,128)}, u32[]{:S(2)}) copy-start(f32[1,3,1,4,32,256]{5,4,3,2,1,0:T(8,128)} %copy-done.36) | copy-start | bytes 1179652
  303.8 36.1 %copy-start.20 = (f32[1,3,1,4,32,256]{5,4,3,2,1,0:T(8,128)}, f32[1,3,1,4,32,256]{5,4,3,2,1,0:T(8,128)S(1)}, u32[]{:S(2)}) copy-start(f32[1,3,1,4,32,256]{5,4,3,2,1,0:T(8,128)S(1)} %get-tuple-element.100) | copy-start | bytes 1179652
  303.8 36.1 %copy-start.23 = (f32[1,3,1,4,32,256]{5,4,3,2,1,0:T(8,128)}, f32[1,3,1,4,32,256]{5,4,3,2,1,0:T(8,128)S(1)}, u32[]{:S(2)}) copy-start(f32[1,3,1,4,32,256]{5,4,3,2,1,0:T(8,128)S(1)} %get-tuple-element.101) | copy-start | bytes 1179652
  323.3 8.1 %collective-permute-start.16 = (f32[1,3,2,1,32,256]{5,4,3,2,1,0:T(8,128)S(1)}, f32[1,3,2,1,32,256]{5,4,3,2,1,0:T(8,128)S(1)}, u32[]{:S(2)}, u32[]{:S(2)}) collective-permute-start(f32[1,3,2,1,32,256]{5,4,3,2,1,0:T(8,128)S(1)} %slice.2254), channel_id=1, source_target_pairs={{2,0},{4,2},{6,4},{8,6},{10,8},{12,10},{14,12},{3,1},{5,3},{7,5},{... | collective-permute-start | bytes 589832 | tf_op jit(solution)/shard_map/ppermute | solution.py:15
  324.6 3.1 collective-permute-start.17
  333.0 5.3 %collective-permute-start.19 = (f32[1,3,2,1,32,256]{5,4,3,2,1,0:T(8,128)S(1)}, f32[1,3,2,1,32,256]{5,4,3,2,1,0:T(8,128)S(1)}, u32[]{:S(2)}, u32[]{:S(2)}) collective-permute-start(f32[1,3,2,1,32,256]{5,4,3,2,1,0:T(8,128)S(1)} %pad_maximum_fusion.25), channel_id=1, source_target_pairs={{0,2},{2,4},{4,6},{6,8},{8,10},{10,12},{12,14},{1,3},{3,5},{5,7},{... | collective-permute-start | bytes 589832 | tf_op jit(solution)/shard_map/ppermute | solution.py:15
  334.6 2.1 collective-permute-start.18
  390.6 23.8 %copy-start.38 = (f32[1,3,1,4,32,256]{5,4,3,2,1,0:T(8,128)}, f32[1,3,1,4,32,256]{5,4,3,2,1,0:T(8,128)S(1)}, u32[]{:S(2)}) copy-start(f32[1,3,1,4,32,256]{5,4,3,2,1,0:T(8,128)S(1)} %get-tuple-element.86) | copy-start | bytes 1179652
  390.7 23.8 %copy-start.40 = (f32[1,3,1,4,32,256]{5,4,3,2,1,0:T(8,128)}, f32[1,3,1,4,32,256]{5,4,3,2,1,0:T(8,128)S(1)}, u32[]{:S(2)}) copy-start(f32[1,3,1,4,32,256]{5,4,3,2,1,0:T(8,128)S(1)} %get-tuple-element.87) | copy-start | bytes 1179652
  393.0 5.0 %collective-permute-start.21 = (f32[1,3,2,4,1,256]{5,4,3,2,1,0:T(1,128)S(1)}, f32[1,3,2,4,1,256]{5,4,3,2,1,0:T(1,128)S(1)}, u32[]{:S(2)}, u32[]{:S(2)}) collective-permute-start(f32[1,3,2,4,1,256]{5,4,3,2,1,0:T(1,128)S(1)} %slice.2299), channel_id=1, source_target_pairs={{1,0},{3,2},{5,4},{7,6},{9,8},{11,10},{13,12},{15,14},{17,16},{19,... | collective-permute-start | bytes 73736 | tf_op jit(solution)/shard_map/ppermute | solution.py:15
  394.3 9.5 %collective-permute-start.20 = (f32[1,3,2,1,32,256]{5,4,3,2,1,0:T(8,128)S(1)}, f32[1,3,2,1,32,256]{5,4,3,2,1,0:T(8,128)S(1)}, u32[]{:S(2)}, u32[]{:S(2)}) collective-permute-start(f32[1,3,2,1,32,256]{5,4,3,2,1,0:T(8,128)S(1)} %slice.2295), channel_id=1, source_target_pairs={{2,0},{4,2},{6,4},{8,6},{10,8},{12,10},{14,12},{3,1},{5,3},{7,5},{... | collective-permute-start | bytes 589832 | tf_op jit(solution)/shard_map/ppermute | solution.py:15
  405.4 6.1 %collective-permute-start.22 = (f32[1,3,2,4,1,256]{5,4,3,2,1,0:T(1,128)S(1)}, f32[1,3,2,4,1,256]{5,4,3,2,1,0:T(1,128)S(1)}, u32[]{:S(2)}, u32[]{:S(2)}) collective-permute-start(f32[1,3,2,4,1,256]{5,4,3,2,1,0:T(1,128)S(1)} %pad_maximum_fusion.35), channel_id=1, source_target_pairs={{0,1},{2,3},{4,5},{6,7},{8,9},{10,11},{12,13},{14,15},{16,17},{18,... | collective-permute-start | bytes 73736 | tf_op jit(solution)/shard_map/ppermute | solution.py:15
  407.5 5.3 %collective-permute-start.23 = (f32[1,3,2,1,32,256]{5,4,3,2,1,0:T(8,128)S(1)}, f32[1,3,2,1,32,256]{5,4,3,2,1,0:T(8,128)S(1)}, u32[]{:S(2)}, u32[]{:S(2)}) collective-permute-start(f32[1,3,2,1,32,256]{5,4,3,2,1,0:T(8,128)S(1)} %pad_maximum_fusion.23), channel_id=1, source_target_pairs={{0,2},{2,4},{4,6},{6,8},{8,10},{10,12},{12,14},{1,3},{3,5},{5,7},{... | collective-permute-start | bytes 589832 | tf_op jit(solution)/shard_map/ppermute | solution.py:15
  (62 other events, 124.9 us)
where the time goes:
time: 472 us; the launch traced here: 469 us
  blocking collectives  181 us (38%)
  between operations  99.9 us (21%)
  other arithmetic  74.5 us (16%)
  waiting for transfers between devices  43.6 us (9%)
  starting transfers between devices  38.4 us (8%)
  local copies, waits for them, and re-layouts  31.8 us (7%)
    psum x3, blocking collectives, body(): lax.psum((product(second, middle), product(second, second), product(sourc...  89.6 us
    psum x2, blocking collectives, body(): lax.psum(product(source, applied), ('gx', 'gy'))  60.3 us
    ppermute x24, waiting for transfers between devices, shifted(): return lax.ppermute(array, axis, pairs)  43.6 us
    ppermute x24, starting transfers between devices, shifted(): return lax.ppermute(array, axis, pairs)  38.4 us
    psum x1, blocking collectives, body(): shadow_dot = lax.psum(product(source, residual), ('gx', 'gy'))  31.3 us
    sub x15, other arithmetic, scaled(): real_part = values[:, :, 0] * real_scale - values[:, :, 1] * imag_scale  27.3 us
    another operation x12, other arithmetic, product(): return jnp.stack([real_part, imag_part])  17.5 us
    unnamed x173, local copies, waits for them, and re-layouts  12.9 us
  transfers between devices with their start and end apart: 24, of which 17 were waited for; matrix products, arithmetic and copies ran while one was open for 2% of the time, Pallas kernels for 0%

commit v1 on v0

--- a/solution.py
+++ b/solution.py
@@ -151,7 +151,7 @@
     solution = jnp.zeros_like(source)
     residual = source
     direction = source
-    shadow_dot = lax.psum(product(source, residual), ("gx", "gy"))
+    shadow_dot = jnp.sum(lax.all_gather(product(source, residual), ("gx", "gy")), axis=0)
     for iteration in range(ITERS):
         applied = operate(direction)
         step_size = complex_ratio(shadow_dot, lax.psum(product(source, applied), ("gx", "gy")))

time: 472 us -> 475 us (level)
    psum x1 -> x0, blocking collectives: 31.3 us -> none  [body(): shadow_dot = lax.psum(product(source, residual), ('gx', 'gy'))]
    unnamed x0 -> x1, blocking collectives: none -> 31.2 us
    unnamed x173 -> x193, local copies, waits for them, and re-layouts: 12.9 us -> 15.4 us
    another operation x12 -> x11, other arithmetic: 17.5 us -> 16 us  [product(): return jnp.stack([real_part, imag_part])]
where the time goes in v1:
time: 475 us; the launch traced here: 472 us
  blocking collectives  181 us (38%)
  between operations  99.5 us (21%)
  other arithmetic  76.3 us (16%)
  waiting for transfers between devices  41.5 us (9%)
  starting transfers between devices  38.4 us (8%)
  local copies, waits for them, and re-layouts  35.3 us (7%)
    psum x3, blocking collectives, body(): lax.psum((product(second, middle), product(second, second), product(sourc...  89.6 us
    psum x2, blocking collectives, body(): lax.psum(product(source, applied), ('gx', 'gy'))  60.3 us
    ppermute x24, waiting for transfers between devices, shifted(): return lax.ppermute(array, axis, pairs)  41.5 us
    ppermute x24, starting transfers between devices, shifted(): return lax.ppermute(array, axis, pairs)  38.4 us
    unnamed x1, blocking collectives  31.2 us
    sub x15, other arithmetic, scaled(): real_part = values[:, :, 0] * real_scale - values[:, :, 1] * imag_scale  27.6 us
    another operation x11, other arithmetic, product(): return jnp.stack([real_part, imag_part])  16 us
    unnamed x193, local copies, waits for them, and re-layouts  15.4 us
  transfers between devices with their start and end apart: 24, of which 17 were waited for; matrix products, arithmetic and copies ran while one was open for 2% of the time, Pallas kernels for 0%

profile of v1, /device:TPU:0, one launch (start us, length us, event | category | flops | bytes accessed | tf_op | source)
XLA Modules:
  0.0 472.0 jit_solution(14484255249574176687)
XLA Ops:
  8.0 6.1 %collective-permute-done = f32[1,3,2,1,32,256]{5,4,3,2,1,0:T(8,128)S(1)} collective-permute-done((f32[1,3,2,1,32,256]{5,4,3,2,1,0:T(8,128)S(1)}, f32[1,3,2,1,32,256]{5,4,3,2,1,0:T(8,128)S(1)}, u32[]{:S(2)}, u32[]{:S(2)}) %collective-permute-start) | collective-permute-done | bytes 196640 | tf_op jit(solution)/shard_map/ppermute | solution.py:15
  16.4 2.1 collective-permute-start.2
  18.6 5.0 %collective-permute-start.3 = (f32[1,3,2,1,32,256]{5,4,3,2,1,0:T(8,128)}, f32[1,3,2,1,32,256]{5,4,3,2,1,0:T(8,128)S(1)}, u32[]{:S(2)}, u32[]{:S(2)}) collective-permute-start(f32[1,3,2,1,32,256]{5,4,3,2,1,0:T(8,128)} %pad_maximum_fusion.33), channel_id=1, source_target_pairs={{0,2},{2,4},{4,6},{6,8},{8,10},{10,12},{12,14},{1,3},{3,5},{5,7},{... | collective-permute-start | bytes 589832 | tf_op jit(solution)/shard_map/ppermute | solution.py:15
  25.4 2.2 collective-permute-done.3
  33.4 1.4 fusion.75
  34.8 31.2 %all-reduce.40 = (f32[32]{0:T(128)S(1)}, f32[2,1]{1,0:T(2,128)S(1)}) all-reduce(f32[32]{0:T(128)S(1)} %fusion.75, f32[2,1]{1,0:T(2,128)S(1)} %pad_maximum_fusion.41), channel_id=2, replica_groups=mesh['groups'=2,'gx'=8,'gy'=2] {'gx','gy'}, use_global_device_ids=true, to_apply=%add.36 | all-reduce | flops 34 | bytes 272
  79.5 1.8 collective-permute-done.5
  81.3 3.2 collective-permute-done.4
  86.0 1.5 collective-permute-start.7
  87.5 1.7 collective-permute-start.6
  99.2 29.5 %all-reduce.39 = (f32[2,1]{1,0:T(2,128)S(1)}, f32[2,1]{1,0:T(2,128)S(1)}, f32[2,1]{1,0:T(2,128)S(1)}) all-reduce(f32[2,1]{1,0:T(2,128)S(1)} %pad_maximum_fusion.42, f32[2,1]{1,0:T(2,128)S(1)} %pad_maximum_fusion.43, f32[2,1]{1,0:T(2,128)S(1)} %pad_maximum_fusion.44), channel_id=1, replica_groups=mesh['groups'=2,'gx'=8,'gy'=2] {'gx','gy'}, use_global_device_ids=true, to_apply=%region_8.0 | all-reduce | flops 6 | bytes 48 | tf_op jit(solution)/shard_map/psum | solution.py:160
  145.3 2.5 multiply_subtract_fusion.11
  170.2 1.8 collective-permute-done.9
  172.0 4.1 collective-permute-done.8
  177.3 1.5 collective-permute-start.11
  187.0 30.3 %psum.81 = f32[2,1]{1,0:T(2,128)S(1)} all-reduce(f32[2,1]{1,0:T(2,128)S(1)} %pad_maximum_fusion.45), channel_id=1, replica_groups=mesh['groups'=2,'gx'=8,'gy'=2] {'gx','gy'}, use_global_device_ids=true, to_apply=%region_17.0 | all-reduce | flops 2 | bytes 16 | tf_op jit(solution)/shard_map/psum | solution.py:157
  226.1 2.6 multiply_subtract_fusion.8
  230.4 1.5 collective-permute-start.13
  231.9 1.6 collective-permute-done.13
  233.5 3.4 collective-permute-done.12
  238.5 1.5 collective-permute-start.15
  240.0 1.5 collective-permute-start.14
  249.2 1.8 pad_maximum_fusion.48
  250.9 1.8 pad_maximum_fusion.47
  252.7 1.8 pad_maximum_fusion.46
  254.5 30.6 %all-reduce.38 = (f32[2,1]{1,0:T(2,128)}, f32[2,1]{1,0:T(2,128)}, f32[2,1]{1,0:T(2,128)}) all-reduce(f32[2,1]{1,0:T(2,128)} %pad_maximum_fusion.46, f32[2,1]{1,0:T(2,128)} %pad_maximum_fusion.47, f32[2,1]{1,0:T(2,128)} %pad_maximum_fusion.48), channel_id=1, replica_groups=mesh['groups'=2,'gx'=8,'gy'=2] {'gx','gy'}, use_global_device_ids=true, to_apply=%region_20.0 | all-reduce | flops 6 | bytes 48 | tf_op jit(solution)/shard_map/psum | solution.py:160
  302.9 2.5 multiply_subtract_fusion.5
  328.6 1.8 collective-permute-done.17
  330.4 3.7 collective-permute-done.16
  335.8 1.5 collective-permute-start.19
  339.4 1.7 collective-permute-done.19
  345.1 2.9 add_reduce_fusion.2
  348.0 1.8 pad_maximum_fusion.49
  349.8 2.2 multiply_subtract_fusion.13
  352.1 30.0 %psum.85 = f32[2,1]{1,0:T(2,128)S(1)} all-reduce(f32[2,1]{1,0:T(2,128)} %pad_maximum_fusion.49), channel_id=1, replica_groups=mesh['groups'=2,'gx'=8,'gy'=2] {'gx','gy'}, use_global_device_ids=true, to_apply=%region_29.0 | all-reduce | flops 2 | bytes 16 | tf_op jit(solution)/shard_map/psum | solution.py:157
  390.5 2.5 multiply_subtract_fusion.2
  393.1 2.3 maximum_subtract_fusion.11
  398.0 2.4 multiply_subtract_fusion.9
  400.4 5.8 %collective-permute-done.20 = f32[1,3,2,1,32,256]{5,4,3,2,1,0:T(8,128)S(1)} collective-permute-done((f32[1,3,2,1,32,256]{5,4,3,2,1,0:T(8,128)S(1)}, f32[1,3,2,1,32,256]{5,4,3,2,1,0:T(8,128)S(1)}, u32[]{:S(2)}, u32[]{:S(2)}) %collective-permute-start.20) | collective-permute-done | bytes 196640 | tf_op jit(solution)/shard_map/ppermute | solution.py:15
  407.9 2.0 collective-permute-start.22
  409.9 1.9 collective-permute-start.23
  411.8 2.3 multiply_subtract_fusion.7
  423.3 2.3 multiply_subtract_fusion.3
  425.6 29.5 %all-reduce.37 = (f32[2,1]{1,0:T(2,128)S(1)}, f32[2,1]{1,0:T(2,128)S(1)}) all-reduce(f32[2,1]{1,0:T(2,128)S(1)} %pad_maximum_fusion.50, f32[2,1]{1,0:T(2,128)S(1)} %pad_maximum_fusion.51), channel_id=1, replica_groups=mesh['groups'=2,'gx'=8,'gy'=2] {'gx','gy'}, use_global_device_ids=true, to_apply=%region_32.0 | all-reduce | flops 4 | bytes 32 | tf_op jit(solution)/shard_map/psum | solution.py:160
  464.1 2.7 multiply_subtract_fusion
  466.8 1.4 multiply_subtract_fusion.1
  468.3 1.5 maximum_subtract_fusion.13
  470.6 1.4 fusion.3
  (461 shorter events, 92.7 us)
Async XLA Ops:
  0.6 7.3 %copy-start.56 = (f32[3,4,32,256]{3,2,1,0:T(8,128)S(1)}, f32[3,4,32,256]{3,2,1,0:T(8,128)}, u32[]{:S(2)}) copy-start(f32[3,4,32,256]{3,2,1,0:T(8,128)} %param.4) | copy-start | bytes 1179652
  1.6 12.5 %collective-permute-start.1 = (f32[1,3,2,4,1,256]{5,4,3,2,1,0:T(1,128)S(1)}, f32[1,3,2,4,1,256]{5,4,3,2,1,0:T(1,128)S(1)}, u32[]{:S(2)}, u32[]{:S(2)}) collective-permute-start(f32[1,3,2,4,1,256]{5,4,3,2,1,0:T(1,128)S(1)} %slice.704), channel_id=1, source_target_pairs={{1,0},{3,2},{5,4},{7,6},{9,8},{11,10},{13,12},{15,14},{17,16},{19,... | collective-permute-start | bytes 73736 | tf_op jit(solution)/shard_map/ppermute | solution.py:15
  3.9 10.2 %collective-permute-start = (f32[1,3,2,1,32,256]{5,4,3,2,1,0:T(8,128)S(1)}, f32[1,3,2,1,32,256]{5,4,3,2,1,0:T(8,128)S(1)}, u32[]{:S(2)}, u32[]{:S(2)}) collective-permute-start(f32[1,3,2,1,32,256]{5,4,3,2,1,0:T(8,128)S(1)} %slice.697), channel_id=1, source_target_pairs={{2,0},{4,2},{6,4},{8,6},{10,8},{12,10},{14,12},{3,1},{5,3},{7,5},{... | collective-permute-start | bytes 589832 | tf_op jit(solution)/shard_map/ppermute | solution.py:15
  7.7 7.2 %copy-start.65 = (f32[4]{0:T(128)}, f32[4]{0:T(128)S(1)}, u32[]{:S(2)}) copy-start(f32[4]{0:T(128)S(1)} %get-tuple-element.430) | copy-start | bytes 52
  7.7 7.2 %copy-start.70 = (f32[4]{0:T(128)}, f32[4]{0:T(128)S(1)}, u32[]{:S(2)}) copy-start(f32[4]{0:T(128)S(1)} %get-tuple-element.431) | copy-start | bytes 52
  8.0 175.3 %copy-start.16 = (f32[3,4,32,256]{3,2,1,0:T(8,128)}, f32[3,4,32,256]{3,2,1,0:T(8,128)S(1)}, u32[]{:S(2)}) copy-start(f32[3,4,32,256]{3,2,1,0:T(8,128)S(1)} %broadcast_multiply_fusion) | copy-start | bytes 1179652
  8.0 7.2 %copy-start.83 = (f32[32]{0:T(128)}, f32[32]{0:T(128)S(1)}, u32[]{:S(2)}) copy-start(f32[32]{0:T(128)S(1)} %get-tuple-element.428) | copy-start | bytes 388
  15.7 8.5 %copy-start.94 = (u32[32]{0:T(128)S(1)}, u32[32]{0:T(128)}, u32[]{:S(2)}) copy-start(u32[32]{0:T(128)} %constant.136) | copy-start | bytes 388
  16.4 9.0 %collective-permute-start.2 = (f32[1,3,2,4,1,256]{5,4,3,2,1,0:T(1,128)S(1)}, f32[1,3,2,4,1,256]{5,4,3,2,1,0:T(1,128)S(1)}, u32[]{:S(2)}, u32[]{:S(2)}) collective-permute-start(f32[1,3,2,4,1,256]{5,4,3,2,1,0:T(1,128)S(1)} %pad_maximum_fusion.40), channel_id=1, source_target_pairs={{0,1},{2,3},{4,5},{6,7},{8,9},{10,11},{12,13},{14,15},{16,17},{18,... | collective-permute-start | bytes 73736 | tf_op jit(solution)/shard_map/ppermute | solution.py:15
  18.6 9.0 %collective-permute-start.3 = (f32[1,3,2,1,32,256]{5,4,3,2,1,0:T(8,128)}, f32[1,3,2,1,32,256]{5,4,3,2,1,0:T(8,128)S(1)}, u32[]{:S(2)}, u32[]{:S(2)}) collective-permute-start(f32[1,3,2,1,32,256]{5,4,3,2,1,0:T(8,128)} %pad_maximum_fusion.33), channel_id=1, source_target_pairs={{0,2},{2,4},{4,6},{6,8},{8,10},{10,12},{12,14},{1,3},{3,5},{5,7},{... | collective-permute-start | bytes 589832 | tf_op jit(solution)/shard_map/ppermute | solution.py:15
  31.0 45.7 %copy-start.27 = (f32[1,3,2,4,32,256]{5,4,3,2,1,0:T(8,128)}, f32[1,3,2,4,32,256]{5,4,3,2,1,0:T(8,128)S(1)}, u32[]{:S(2)}) copy-start(f32[1,3,2,4,32,256]{5,4,3,2,1,0:T(8,128)S(1)} %maximum_subtract_fusion) | copy-start | bytes 2359300
  76.8 7.6 %collective-permute-start.4 = (f32[1,3,2,1,32,256]{5,4,3,2,1,0:T(8,128)S(1)}, f32[1,3,2,1,32,256]{5,4,3,2,1,0:T(8,128)S(1)}, u32[]{:S(2)}, u32[]{:S(2)}) collective-permute-start(f32[1,3,2,1,32,256]{5,4,3,2,1,0:T(8,128)S(1)} %slice.2129), channel_id=1, source_target_pairs={{2,0},{4,2},{6,4},{8,6},{10,8},{12,10},{14,12},{3,1},{5,3},{7,5},{... | collective-permute-start | bytes 589832 | tf_op jit(solution)/shard_map/ppermute | solution.py:15
  78.2 3.1 collective-permute-start.5
  86.0 6.0 %collective-permute-start.7 = (f32[1,3,2,1,32,256]{5,4,3,2,1,0:T(8,128)S(1)}, f32[1,3,2,1,32,256]{5,4,3,2,1,0:T(8,128)S(1)}, u32[]{:S(2)}, u32[]{:S(2)}) collective-permute-start(f32[1,3,2,1,32,256]{5,4,3,2,1,0:T(8,128)S(1)} %pad_maximum_fusion.31), channel_id=1, source_target_pairs={{0,2},{2,4},{4,6},{6,8},{8,10},{10,12},{12,14},{1,3},{3,5},{5,7},{... | collective-permute-start | bytes 589832 | tf_op jit(solution)/shard_map/ppermute | solution.py:15
  87.5 4.5 collective-permute-start.6
  128.7 19.0 %copy-start.29 = (f32[1,3,2,4,32,256]{5,4,3,2,1,0:T(8,128)S(1)}, f32[1,3,2,4,32,256]{5,4,3,2,1,0:T(8,128)}, u32[]{:S(2)}) copy-start(f32[1,3,2,4,32,256]{5,4,3,2,1,0:T(8,128)} %copy-done.28) | copy-start | bytes 2359300
  149.1 34.2 %copy-start.1 = (f32[1,3,1,4,32,256]{5,4,3,2,1,0:T(8,128)}, f32[1,3,1,4,32,256]{5,4,3,2,1,0:T(8,128)S(1)}, u32[]{:S(2)}) copy-start(f32[1,3,1,4,32,256]{5,4,3,2,1,0:T(8,128)S(1)} %get-tuple-element.131) | copy-start | bytes 1179652
  167.2 16.1 %copy-start.34 = (f32[1,3,1,4,32,256]{5,4,3,2,1,0:T(8,128)}, f32[1,3,1,4,32,256]{5,4,3,2,1,0:T(8,128)S(1)}, u32[]{:S(2)}) copy-start(f32[1,3,1,4,32,256]{5,4,3,2,1,0:T(8,128)S(1)} %get-tuple-element.132) | copy-start | bytes 1179652
  167.2 16.1 %copy-start.36 = (f32[1,3,1,4,32,256]{5,4,3,2,1,0:T(8,128)}, f32[1,3,1,4,32,256]{5,4,3,2,1,0:T(8,128)S(1)}, u32[]{:S(2)}) copy-start(f32[1,3,1,4,32,256]{5,4,3,2,1,0:T(8,128)S(1)} %get-tuple-element.133) | copy-start | bytes 1179652
  167.5 9.1 %copy-start.5 = (f32[1,3,2,4,32,256]{5,4,3,2,1,0:T(8,128)}, f32[1,3,2,4,32,256]{5,4,3,2,1,0:T(8,128)S(1)}, u32[]{:S(2)}) copy-start(f32[1,3,2,4,32,256]{5,4,3,2,1,0:T(8,128)S(1)} %maximum_add_fusion.1) | copy-start | bytes 2359300
  167.6 8.6 %collective-permute-start.8 = (f32[1,3,2,1,32,256]{5,4,3,2,1,0:T(8,128)S(1)}, f32[1,3,2,1,32,256]{5,4,3,2,1,0:T(8,128)S(1)}, u32[]{:S(2)}, u32[]{:S(2)}) collective-permute-start(f32[1,3,2,1,32,256]{5,4,3,2,1,0:T(8,128)S(1)} %slice.2172), channel_id=1, source_target_pairs={{2,0},{4,2},{6,4},{8,6},{10,8},{12,10},{14,12},{3,1},{5,3},{7,5},{... | collective-permute-start | bytes 589832 | tf_op jit(solution)/shard_map/ppermute | solution.py:15
  168.9 3.1 collective-permute-start.9
  177.3 4.9 %collective-permute-start.11 = (f32[1,3,2,1,32,256]{5,4,3,2,1,0:T(8,128)S(1)}, f32[1,3,2,1,32,256]{5,4,3,2,1,0:T(8,128)S(1)}, u32[]{:S(2)}, u32[]{:S(2)}) collective-permute-start(f32[1,3,2,1,32,256]{5,4,3,2,1,0:T(8,128)S(1)} %pad_maximum_fusion.29), channel_id=1, source_target_pairs={{0,2},{2,4},{4,6},{6,8},{8,10},{10,12},{12,14},{1,3},{3,5},{5,7},{... | collective-permute-start | bytes 589832 | tf_op jit(solution)/shard_map/ppermute | solution.py:15
  178.8 2.1 collective-permute-start.10
  217.2 11.5 %copy-start.2 = (f32[1,3,1,4,32,256]{5,4,3,2,1,0:T(8,128)S(1)}, f32[1,3,1,4,32,256]{5,4,3,2,1,0:T(8,128)}, u32[]{:S(2)}) copy-start(f32[1,3,1,4,32,256]{5,4,3,2,1,0:T(8,128)} %copy-done.1) | copy-start | bytes 1179652
  228.7 17.0 %copy-start.9 = (f32[1,3,1,4,32,256]{5,4,3,2,1,0:T(8,128)}, f32[1,3,1,4,32,256]{5,4,3,2,1,0:T(8,128)S(1)}, u32[]{:S(2)}) copy-start(f32[1,3,1,4,32,256]{5,4,3,2,1,0:T(8,128)S(1)} %get-tuple-element.118) | copy-start | bytes 1179652
  228.7 17.0 %copy-start.12 = (f32[1,3,1,4,32,256]{5,4,3,2,1,0:T(8,128)}, f32[1,3,1,4,32,256]{5,4,3,2,1,0:T(8,128)S(1)}, u32[]{:S(2)}) copy-start(f32[1,3,1,4,32,256]{5,4,3,2,1,0:T(8,128)S(1)} %get-tuple-element.119) | copy-start | bytes 1179652
  229.1 7.8 %collective-permute-start.12 = (f32[1,3,2,1,32,256]{5,4,3,2,1,0:T(8,128)S(1)}, f32[1,3,2,1,32,256]{5,4,3,2,1,0:T(8,128)S(1)}, u32[]{:S(2)}, u32[]{:S(2)}) collective-permute-start(f32[1,3,2,1,32,256]{5,4,3,2,1,0:T(8,128)S(1)} %slice.2213), channel_id=1, source_target_pairs={{2,0},{4,2},{6,4},{8,6},{10,8},{12,10},{14,12},{3,1},{5,3},{7,5},{... | collective-permute-start | bytes 589832 | tf_op jit(solution)/shard_map/ppermute | solution.py:15
  230.4 3.1 collective-permute-start.13
  238.5 5.7 %collective-permute-start.15 = (f32[1,3,2,1,32,256]{5,4,3,2,1,0:T(8,128)S(1)}, f32[1,3,2,1,32,256]{5,4,3,2,1,0:T(8,128)S(1)}, u32[]{:S(2)}, u32[]{:S(2)}) collective-permute-start(f32[1,3,2,1,32,256]{5,4,3,2,1,0:T(8,128)S(1)} %pad_maximum_fusion.27), channel_id=1, source_target_pairs={{0,2},{2,4},{4,6},{6,8},{8,10},{10,12},{12,14},{1,3},{3,5},{5,7},{... | collective-permute-start | bytes 589832 | tf_op jit(solution)/shard_map/ppermute | solution.py:15
  240.0 3.9 collective-permute-start.14
  285.1 20.4 %copy-start.31 = (f32[1,3,2,4,32,256]{5,4,3,2,1,0:T(8,128)S(1)}, f32[1,3,2,4,32,256]{5,4,3,2,1,0:T(8,128)}, u32[]{:S(2)}) copy-start(f32[1,3,2,4,32,256]{5,4,3,2,1,0:T(8,128)} %copy-done.30) | copy-start | bytes 2359300
  302.9 21.0 %copy-start.3 = (f32[1,3,1,4,32,256]{5,4,3,2,1,0:T(8,128)S(1)}, f32[1,3,1,4,32,256]{5,4,3,2,1,0:T(8,128)}, u32[]{:S(2)}) copy-start(f32[1,3,1,4,32,256]{5,4,3,2,1,0:T(8,128)} %copy-done.1) | copy-start | bytes 1179652
  302.9 21.0 %copy-start.35 = (f32[1,3,1,4,32,256]{5,4,3,2,1,0:T(8,128)S(1)}, f32[1,3,1,4,32,256]{5,4,3,2,1,0:T(8,128)}, u32[]{:S(2)}) copy-start(f32[1,3,1,4,32,256]{5,4,3,2,1,0:T(8,128)} %copy-done.34) | copy-start | bytes 1179652
  302.9 21.0 %copy-start.37 = (f32[1,3,1,4,32,256]{5,4,3,2,1,0:T(8,128)S(1)}, f32[1,3,1,4,32,256]{5,4,3,2,1,0:T(8,128)}, u32[]{:S(2)}) copy-start(f32[1,3,1,4,32,256]{5,4,3,2,1,0:T(8,128)} %copy-done.36) | copy-start | bytes 1179652
  306.8 35.9 %copy-start.20 = (f32[1,3,1,4,32,256]{5,4,3,2,1,0:T(8,128)}, f32[1,3,1,4,32,256]{5,4,3,2,1,0:T(8,128)S(1)}, u32[]{:S(2)}) copy-start(f32[1,3,1,4,32,256]{5,4,3,2,1,0:T(8,128)S(1)} %get-tuple-element.100) | copy-start | bytes 1179652
  306.8 35.9 %copy-start.23 = (f32[1,3,1,4,32,256]{5,4,3,2,1,0:T(8,128)}, f32[1,3,1,4,32,256]{5,4,3,2,1,0:T(8,128)S(1)}, u32[]{:S(2)}) copy-start(f32[1,3,1,4,32,256]{5,4,3,2,1,0:T(8,128)S(1)} %get-tuple-element.101) | copy-start | bytes 1179652
  326.0 8.7 %copy-start.7 = (f32[1,3,2,4,32,256]{5,4,3,2,1,0:T(8,128)}, f32[1,3,2,4,32,256]{5,4,3,2,1,0:T(8,128)S(1)}, u32[]{:S(2)}) copy-start(f32[1,3,2,4,32,256]{5,4,3,2,1,0:T(8,128)S(1)} %maximum_add_fusion.2) | copy-start | bytes 2359300
  326.0 8.1 %collective-permute-start.16 = (f32[1,3,2,1,32,256]{5,4,3,2,1,0:T(8,128)S(1)}, f32[1,3,2,1,32,256]{5,4,3,2,1,0:T(8,128)S(1)}, u32[]{:S(2)}, u32[]{:S(2)}) collective-permute-start(f32[1,3,2,1,32,256]{5,4,3,2,1,0:T(8,128)S(1)} %slice.2256), channel_id=1, source_target_pairs={{2,0},{4,2},{6,4},{8,6},{10,8},{12,10},{14,12},{3,1},{5,3},{7,5},{... | collective-permute-start | bytes 589832 | tf_op jit(solution)/shard_map/ppermute | solution.py:15
  327.3 3.1 collective-permute-start.17
  335.8 5.3 %collective-permute-start.19 = (f32[1,3,2,1,32,256]{5,4,3,2,1,0:T(8,128)S(1)}, f32[1,3,2,1,32,256]{5,4,3,2,1,0:T(8,128)S(1)}, u32[]{:S(2)}, u32[]{:S(2)}) collective-permute-start(f32[1,3,2,1,32,256]{5,4,3,2,1,0:T(8,128)S(1)} %pad_maximum_fusion.25), channel_id=1, source_target_pairs={{0,2},{2,4},{4,6},{6,8},{8,10},{10,12},{12,14},{1,3},{3,5},{5,7},{... | collective-permute-start | bytes 589832 | tf_op jit(solution)/shard_map/ppermute | solution.py:15
  337.3 2.1 collective-permute-start.18
  393.1 23.8 %copy-start.38 = (f32[1,3,1,4,32,256]{5,4,3,2,1,0:T(8,128)}, f32[1,3,1,4,32,256]{5,4,3,2,1,0:T(8,128)S(1)}, u32[]{:S(2)}) copy-start(f32[1,3,1,4,32,256]{5,4,3,2,1,0:T(8,128)S(1)} %get-tuple-element.86) | copy-start | bytes 1179652
  393.1 23.8 %copy-start.40 = (f32[1,3,1,4,32,256]{5,4,3,2,1,0:T(8,128)}, f32[1,3,1,4,32,256]{5,4,3,2,1,0:T(8,128)S(1)}, u32[]{:S(2)}) copy-start(f32[1,3,1,4,32,256]{5,4,3,2,1,0:T(8,128)S(1)} %get-tuple-element.87) | copy-start | bytes 1179652
  395.4 5.0 %collective-permute-start.21 = (f32[1,3,2,4,1,256]{5,4,3,2,1,0:T(1,128)S(1)}, f32[1,3,2,4,1,256]{5,4,3,2,1,0:T(1,128)S(1)}, u32[]{:S(2)}, u32[]{:S(2)}) collective-permute-start(f32[1,3,2,4,1,256]{5,4,3,2,1,0:T(1,128)S(1)} %slice.2301), channel_id=1, source_target_pairs={{1,0},{3,2},{5,4},{7,6},{9,8},{11,10},{13,12},{15,14},{17,16},{19,... | collective-permute-start | bytes 73736 | tf_op jit(solution)/shard_map/ppermute | solution.py:15
  396.7 9.5 %collective-permute-start.20 = (f32[1,3,2,1,32,256]{5,4,3,2,1,0:T(8,128)S(1)}, f32[1,3,2,1,32,256]{5,4,3,2,1,0:T(8,128)S(1)}, u32[]{:S(2)}, u32[]{:S(2)}) collective-permute-start(f32[1,3,2,1,32,256]{5,4,3,2,1,0:T(8,128)S(1)} %slice.2297), channel_id=1, source_target_pairs={{2,0},{4,2},{6,4},{8,6},{10,8},{12,10},{14,12},{3,1},{5,3},{7,5},{... | collective-permute-start | bytes 589832 | tf_op jit(solution)/shard_map/ppermute | solution.py:15
  407.9 6.2 %collective-permute-start.22 = (f32[1,3,2,4,1,256]{5,4,3,2,1,0:T(1,128)S(1)}, f32[1,3,2,4,1,256]{5,4,3,2,1,0:T(1,128)S(1)}, u32[]{:S(2)}, u32[]{:S(2)}) collective-permute-start(f32[1,3,2,4,1,256]{5,4,3,2,1,0:T(1,128)S(1)} %pad_maximum_fusion.35), channel_id=1, source_target_pairs={{0,1},{2,3},{4,5},{6,7},{8,9},{10,11},{12,13},{14,15},{16,17},{18,... | collective-permute-start | bytes 73736 | tf_op jit(solution)/shard_map/ppermute | solution.py:15
  409.9 5.3 %collective-permute-start.23 = (f32[1,3,2,1,32,256]{5,4,3,2,1,0:T(8,128)S(1)}, f32[1,3,2,1,32,256]{5,4,3,2,1,0:T(8,128)S(1)}, u32[]{:S(2)}, u32[]{:S(2)}) collective-permute-start(f32[1,3,2,1,32,256]{5,4,3,2,1,0:T(8,128)S(1)} %pad_maximum_fusion.23), channel_id=1, source_target_pairs={{0,2},{2,4},{4,6},{6,8},{8,10},{10,12},{12,14},{1,3},{3,5},{5,7},{... | collective-permute-start | bytes 589832 | tf_op jit(solution)/shard_map/ppermute | solution.py:15
  (71 other events, 105.0 us)
